TPU v7x, 32 devices: a whole 2x2x4 slice. The times are simulated.
32 devices in a mesh: seq: 16 (over z, y, x), tp: 2 (over core).
Axes of the slice: x: 2, y: 2, z: 4, core: 2. Of those that a mesh axis runs over, the one named last changes fastest.
Arguments:
- img: bfloat16 [4, 512, 3072], P(None, 'seq', 'tp'), may hold values from -6 to 6
- txt: bfloat16 [4, 64, 3072], P(None, 'seq', 'tp'), may hold values from -6 to 6
- prev_mod: bfloat16 [4, 512, 3072], P(None, 'seq', 'tp'), may hold values from -47 to 47
- cache: float32 [4, 512, 3072], P(None, 'seq', 'tp'), may hold values from -6 to 6
- modulation: bfloat16 [3, 4, 3072], P(None, None, 'tp'), may hold values from -4 to 4
- w_qkv: bfloat16 [3072, 3, 2048], P('seq', None, 'tp'), may hold values from -1 to 1, as said below
- qk_gain: float32 [2, 2048], P(None, 'tp'), may hold values from 0.5 to 6, as said below
- output_weight: bfloat16 [2048, 3072], P('tp'), may hold values from -0.1875 to 0.1875
- text_len: int32 [4], replicated, may hold values from 1 to 64
- refresh: int32 [4], replicated, may hold values from 0 to 1, as said below
Outputs:
- out_img: float32 [4, 512, 3072], P(None, 'seq', 'tp')
- new_cache: float32 [4, 512, 3072], P(None, 'seq', 'tp')
- rel_l1: float32 [4], replicated
Inputs may be any that keep to these rules, and one draw needn't show every extreme that they name: `refresh`: at least one sequence has flag 1 and at least one has flag 0. `w_qkv`: entries of spread about one over the square root of 3072. `qk_gain`: positive.
All inputs are finite; a program needn't handle non-finite values.
Results may differ from a plain program's by a relative error of at most 0.013.
The roundings to bfloat16 on the way count: a program that leaves them out, or rounds other values in their place, can miss the bound.
Values may be sent and summed in bfloat16 or wider, within the bound.
A program may use at most 128 MiB of HBM per device.

v0:
```python
import jax
import jax.numpy as jnp
from jax import lax
from jax.sharding import PartitionSpec as P

HD = 128
EPS = 0.1
NEG = -1e30


def unit_heads(block, gain):
    shaped = block.reshape(block.shape[:-1] + (block.shape[-1] // HD, HD))
    scaled = shaped * lax.rsqrt(jnp.mean(jnp.square(shaped), axis=-1, keepdims=True) + EPS)
    return scaled.reshape(block.shape) * gain


def local(img, txt, prev_mod, cache, modulation, w_qkv, qk_gain, output_weight, text_len, refresh):
    batch, img_rows, width_loc = img.shape
    txt_rows = txt.shape[1]
    rows = txt_rows + img_rows
    joined = jnp.concatenate([txt, img], axis=1)
    local_mods = modulation.astype(jnp.float32)
    wide, wide_mod = (
        lax.all_gather(joined, "tp", axis=2, tiled=True),
        lax.all_gather(modulation, "tp", axis=2, tiled=True),
    )
    wide_mods = wide_mod.astype(jnp.float32)
    values = wide.astype(jnp.float32)
    center = jnp.mean(values, axis=2, keepdims=True)
    spread = jnp.mean(jnp.square(values - center), axis=2, keepdims=True)
    normed = (values - center) * lax.rsqrt(spread + EPS)
    modded = (normed * (1.0 + wide_mods[1][:, None, :]) + wide_mods[0][:, None, :]).astype(
        jnp.bfloat16
    )
    offset = lax.axis_index("tp") * width_loc
    own_image = lax.dynamic_slice_in_dim(modded[:, txt_rows:, :], offset, width_loc, 2)
    previous = prev_mod.astype(jnp.float32)
    gap = jnp.sum(jnp.abs(own_image.astype(jnp.float32) - previous), axis=(1, 2))
    base_sum = jnp.sum(jnp.abs(previous), axis=(1, 2))
    numer, denom = lax.psum((gap, base_sum), ("seq", "tp"))
    rel_l1 = numer / jnp.maximum(denom, 1.0)
    columns = w_qkv.shape[2]
    projected = jnp.einsum(
        "btd,dkc->btkc",
        modded,
        lax.all_gather(w_qkv, "seq", axis=0, tiled=True),
        preferred_element_type=jnp.float32,
    )
    heads = columns // HD
    query = unit_heads(projected[:, txt_rows:, 0, :], qk_gain[0]).astype(jnp.bfloat16)
    query_heads = query.reshape(batch, img_rows, heads, HD)
    keyed = unit_heads(projected[:, :, 1, :], qk_gain[1]).astype(jnp.bfloat16)
    valued = projected[:, :, 2, :].astype(jnp.bfloat16)
    paired = jnp.stack([keyed, valued], axis=2)
    score_scale = 1.0 / HD**0.5
    start_top = jnp.full((batch, heads, img_rows), NEG, jnp.float32)
    piece = lax.all_gather(paired, "seq", axis=1, tiled=True)
    top = start_top
    count = piece.shape[1]
    index = jnp.arange(count, dtype=jnp.int32)
    slot = index % rows
    text_pos = index // rows * txt_rows + slot
    valid = (slot >= txt_rows)[None, :] | (text_pos[None, :] < text_len[:, None])
    keys = piece[:, :, 0, :].reshape(batch, count, heads, HD)
    vals = piece[:, :, 1, :].reshape(batch, count, heads, HD)
    logit_scores = (
        jnp.einsum("bqhc,bkhc->bhqk", query_heads, keys, preferred_element_type=jnp.float32)
        * score_scale
    )
    logit_scores = jnp.where(valid[:, None, None, :], logit_scores, NEG)
    new_top = jnp.maximum(top, jnp.max(logit_scores, axis=3))
    attention_weights = jnp.where(
        valid[:, None, None, :], jnp.exp(logit_scores - new_top[..., None]), 0.0
    )
    total = jnp.sum(attention_weights, axis=3)
    summed_output = jnp.einsum(
        "bhqk,bkhc->bhqc",
        attention_weights.astype(jnp.bfloat16),
        vals,
        preferred_element_type=jnp.float32,
    )
    top, total, summed_output = (new_top, total, summed_output)
    attended_values = (summed_output / total[..., None]).astype(jnp.bfloat16)
    attended_values = attended_values.transpose(0, 2, 1, 3).reshape(batch, img_rows, columns)
    partial_output = jnp.einsum(
        "pxr,ro->pxo", attended_values, output_weight, preferred_element_type=jnp.float32
    )
    whole = lax.psum(partial_output.astype(jnp.bfloat16), "tp").astype(jnp.float32)
    mixed_heads = lax.dynamic_slice_in_dim(whole, lax.axis_index("tp") * width_loc, width_loc, 2)
    resid = local_mods[2][:, None, :] * mixed_heads
    flag = (refresh == 1)[:, None, None]
    new_cache = jnp.where(flag, resid, cache)
    out_img = img.astype(jnp.float32) + new_cache
    return (out_img, new_cache, rel_l1)


def solution(mesh):
    return jax.shard_map(
        local,
        mesh=mesh,
        in_specs=(
            P(None, "seq", "tp"),
            P(None, "seq", "tp"),
            P(None, "seq", "tp"),
            P(None, "seq", "tp"),
            P(None, None, "tp"),
            P("seq", None, "tp"),
            P(None, "tp"),
            P("tp", None),
            P(),
            P(),
        ),
        out_specs=(P(None, "seq", "tp"), P(None, "seq", "tp"), P()),
        check_vma=False,
    )
```

profile of v0, /device:TPU:0, one launch (start us, length us, event | category | flops | bytes accessed | tf_op | source)
XLA Modules:
  0.0 434.7 jit_solution(10169232465015273428)
XLA Ops:
  7.2 0.0 all-gather.3.cloned.1.call-start
  7.2 0.7 all-gather.3.cloned.1.call-update
  7.9 0.0 all-gather.5.cloned.1.call-start
  8.0 2.2 all_gather.13
  10.2 1.1 pad_maximum_fusion.1
  11.3 2.5 all_gather.12
  13.8 0.2 convert_reduce_fusion
  14.1 0.4 fusion.14
  14.5 0.5 fusion.17
  15.0 209.3 %all-gather.3.cloned.1.call-done = bf16[3072,3,1024]{2,0,1:T(8,128)(2,1)} async-done(((bf16[192,3,1024]{2,0,1:T(8,128)(2,1)}), bf16[3072,3,1024]{2,0,1:T(8,128)(2,1)}) %all-gather.3.cloned.1.call-update) | async-done | bytes 18874384 | tf_op jit(solution)/shard_map/all_gather | solution.py:46
  224.3 8.1 %fusion = f32[4,36,3,1024]{3,1,2,0:T(8,128)S(1)} fusion(bf16[3072,3,1024]{2,0,1:T(8,128)(2,1)} %all-gather.3.cloned.1.call-done, bf16[4,36,3072]{2,1,0:T(8,128)(2,1)S(1)} %fusion.17), kind=kOutput, calls=%fused_computation | convolution fusion | flops 2717908992 | bytes 21528576 | tf_op jit(solution)/shard_map/btd,dkc->btkc/dot_general | solution.py:43
  232.4 0.9 slice_multiply_fusion
  233.3 0.8 slice.62
  234.1 1.2 reshape.130
  235.3 0.9 reduce_sum.66
  236.1 1.0 copy.47
  237.1 0.1 copy.48
  237.2 1.0 mul.103
  238.3 1.3 mul.104
  239.5 0.4 fusion.51
  239.9 0.0 copy-start.2
  239.9 1.1 pad_maximum_fusion
  241.0 1.3 copy.50
  242.3 0.0 all-gather.5.cloned.1.call-update
  242.3 0.0 all-reduce.3.cloned.1.call-start
  242.4 1.1 slice.53
  243.5 1.3 fusion.49
  244.8 40.5 %all-reduce = (f32[4]{0:T(128)S(1)}, f32[4]{0:T(128)S(1)}) all-reduce(f32[4]{0:T(128)S(1)} %get-tuple-element.4, f32[4]{0:T(128)S(1)} %get-tuple-element.3), channel_id=1, replica_groups=mesh['seq'=16,'tp'=2] {'seq','tp'}, use_global_device_ids=true, to_apply=%region_8.9 | all-reduce | flops 8 | bytes 64 | tf_op jit(solution)/shard_map/psum | solution.py:40
  285.3 0.1 compare_or_fusion
  285.4 0.1 slice.48
  285.5 0.1 copy.66
  285.6 0.2 fusion.52
  285.8 0.2 fusion.54
  286.0 77.3 %all-gather.5.cloned.1.call-done = bf16[4,576,2,1024]{3,0,2,1:T(4,128)(2,1)} async-done(((bf16[4,36,2,1024]{3,0,2,1:T(4,128)(2,1)}), bf16[4,576,2,1024]{3,0,2,1:T(4,128)(2,1)}) %all-gather.5.cloned.1.call-update) | async-done | bytes 9437200 | tf_op jit(solution)/shard_map/all_gather | solution.py:57
  363.3 10.7 %fusion.70 = (bf16[4,576,1,1024]{3,0,2,1:T(4,128)(2,1)}, bf16[4,576,1,1024]{3,0,2,1:T(4,128)(2,1)}) fusion(bf16[4,576,2,1024]{3,0,2,1:T(4,128)(2,1)} %all-gather.5.cloned.1.call-done), kind=kLoop, calls=%fused_computation.82 | loop fusion | bytes 18874368 | tf_op jit(solution)/shard_map/slice | solution.py:64
  374.0 8.0 %reshape.131 = bf16[4,576,8,128]{3,2,0,1:T(8,128)(2,1)} reshape(bf16[4,576,1,1024]{3,0,2,1:T(4,128)(2,1)} %get-tuple-element.9) | data formatting | bytes 9437184 | tf_op jit(solution)/shard_map/reshape;squeeze | solution.py:64
  382.0 7.5 %fusion.13 = (f32[4,8,32]{2,1,0:T(8,128)S(1)}, f32[4,8,32,576]{3,2,1,0:T(8,128)S(1)}) fusion(pred[4,576]{1,0:T(4,128)(4,1)S(1)} %compare_or_fusion, bf16[4,576,8,128]{3,2,0,1:T(8,128)(2,1)} %reshape.131, bf16[4,32,8,128]{3,2,1,0:T(8,128)(2,1)S(1)} %fusion.54), kind=kOutput, calls=%fused_computation.15 | convolution fusion | flops 152763392 | bytes 7346432 | tf_op jit(solution)/shard_map/bqhc,bkhc->bhqk/dot_general | solution.py:67
  389.5 8.0 %reshape.132 = bf16[4,576,8,128]{3,2,0,1:T(8,128)(2,1)} reshape(bf16[4,576,1,1024]{3,0,2,1:T(4,128)(2,1)} %get-tuple-element.10) | data formatting | bytes 9437184 | tf_op jit(solution)/shard_map/reshape;squeeze | solution.py:65
  397.6 0.8 fusion.18
  398.4 0.0 slice-start.1
  398.4 8.1 %fusion.41 = bf16[4,8,4,8,128]{4,3,2,1,0:T(8,128)(2,1)S(1)} fusion(bf16[4,576,8,128]{3,2,0,1:T(8,128)(2,1)} %reshape.132, f32[4,8,32,576]{3,2,1,0:T(8,128)S(1)} %get-tuple-element.16, f32[4,8,32]{2,1,0:T(8,128)S(1)} %broadcast_maximum_fusion, pred[4,576]{1,0:T(4,128)(4,1)S(1)} %compare_or_fusion, f32[4,32,8]{1,2,0:T(8,128)S(1)} %bitcast.67), kind=kOutput, calls=%fused_computation.30 | convolution fusion | flops 154206208 | bytes 7350528 | tf_op jit(solution)/shard_map/bhqk,bkhc->bhqc/dot_general | solution.py:76
  406.6 0.0 copy-start.1
  406.6 1.9 fusion.8
  408.4 0.0 all-reduce.3.cloned.1.call-update
  408.5 0.5 maximum_divide_fusion
  409.0 0.7 bitcast_convert_fusion
  409.7 16.1 %all-reduce.3.cloned.1.call-done = bf16[4,32,3072]{2,1,0:T(8,128)(2,1)} async-done(((bf16[4,32,3072]{2,1,0:T(8,128)(2,1)}), bf16[4,32,3072]{2,1,0:T(8,128)(2,1)}) %all-reduce.3.cloned.1.call-update) | async-done | bytes 786448 | tf_op jit(solution)/shard_map/psum | solution.py:88
  425.8 2.4 convert_add_fusion
  (25 shorter events, 0.1 us)
Async XLA Ops:
  7.2 217.1 %all-gather.3.cloned.1.call-start = ((), (), s32[]{:S(2)}) async-start(), calls=%async_computation | async-start | bytes 20054016 | tf_op jit(solution)/shard_map/all_gather | solution.py:46
  7.9 6.6 %copy-start.3 = (f32[2,1024]{1,0:T(2,128)S(1)}, f32[2,1024]{1,0:T(2,128)}, u32[]{:S(2)}) copy-start(f32[2,1024]{1,0:T(2,128)} %param.16) | copy-start | bytes 24580
  7.9 355.4 %all-gather.5.cloned.1.call-start = ((), (), s32[]{:S(2)}) async-start(), calls=%async_computation.1 | async-start | bytes 10027008 | tf_op jit(solution)/shard_map/all_gather | solution.py:57
  239.9 3.6 copy-start.2
  239.9 45.4 %copy-start.4 = (s32[4]{0:T(128)S(1)}, s32[4]{0:T(128)}, u32[]{:S(2)}) copy-start(s32[4]{0:T(128)} %param.18) | copy-start | bytes 52
  242.3 183.5 %all-reduce.3.cloned.1.call-start = ((), (), s32[]{:S(2)}) async-start(), calls=%async_computation.2 | async-start | bytes 1572864 | tf_op jit(solution)/shard_map/psum | solution.py:88
  397.6 8.9 %slice-start = ((s8[6291456]{0:T(1024)(128)(4,1)}), s8[4194304]{0:T(1024)(128)(4,1)S(1)}, s32[]{:S(2)}) async-start(s8[6291456]{0:T(1024)(128)(4,1)} %bitcast.62), calls=%async_computation.3 | async-start | bytes 8388608
  398.4 8.1 %slice-start.1 = ((s8[6291456]{0:T(1024)(128)(4,1)}), s8[2097152]{0:T(1024)(128)(4,1)S(1)}, s32[]{:S(2)}) async-start(s8[6291456]{0:T(1024)(128)(4,1)} %bitcast.62), calls=%async_computation.4 | async-start | bytes 4194304
  406.5 1.9 copy-start.5
  406.5 19.2 %copy-start = (bf16[4,32,1536]{2,1,0:T(8,128)(2,1)S(1)}, bf16[4,32,1536]{2,1,0:T(8,128)(2,1)}, u32[]{:S(2)}) copy-start(bf16[4,32,1536]{2,1,0:T(8,128)(2,1)} %param.10) | copy-start | bytes 1179652
  406.6 19.2 %copy-start.1 = (f32[4,32,1536]{2,1,0:T(8,128)S(1)}, f32[4,32,1536]{2,1,0:T(8,128)}, u32[]{:S(2)}) copy-start(f32[4,32,1536]{2,1,0:T(8,128)} %param.13) | copy-start | bytes 2359300
Sparse Core Ops, SparseCore 0:
  10.6 213.6 all-gather.2
  242.4 120.8 all-gather.4
  408.6 17.1 all-reduce.2
where the time goes:
time: 436 us; the launch traced here: 435 us
  waiting for transfers between devices  303 us (69%)
  blocking collectives  45.3 us (10%)
  local copies, waits for them, and re-layouts  34.7 us (8%)
  matrix products  25.6 us (6%)
  between operations  14 us (3%)
  other arithmetic  11.8 us (3%)
    all_gather x1, waiting for transfers between devices, local(): lax.all_gather(w_qkv, 'seq', axis=0, tiled=True)  209 us
    all_gather x1, waiting for transfers between devices, local(): piece = lax.all_gather(paired, 'seq', axis=1, tiled=True)  77.3 us
    psum x1, blocking collectives, local(): numer, denom = lax.psum((gap, base_sum), ('seq', 'tp'))  40.5 us
    psum x1, waiting for transfers between devices, local(): lax.psum(partial_output.astype(jnp.bfloat16), 'tp').astype(jnp.float32)  16.1 us
    slice x1, local copies, waits for them, and re-layouts, local(): keys = piece[:, :, 0, :].reshape(batch, count, heads, HD)  10.7 us
  transfers between devices with their start and end apart: 3, of which 3 were waited for; matrix products, arithmetic and copies ran while one was open for 2% of the time, Pallas kernels for 0%

commit v1 on v0

--- a/solution.py
+++ b/solution.py
@@ -43,7 +43,9 @@
     projected = jnp.einsum(
         "btd,dkc->btkc",
         modded,
-        lax.all_gather(w_qkv, "seq", axis=0, tiled=True),
+        jnp.concatenate(
+            lax.all_to_all(jnp.stack([w_qkv] * lax.axis_size("seq")), "seq", 0, 0), axis=0
+        ),
         preferred_element_type=jnp.float32,
     )
     heads = columns // HD

time: 436 us -> 671 us (1.54)
  waiting for transfers between devices: 303 us -> 445 us
  blocking collectives: 45.3 us -> 121 us
  local copies, waits for them, and re-layouts: 34.7 us -> 51.9 us
  starting transfers between devices: 0.12 us -> 8.61 us
  matrix products: 25.6 us -> 18.6 us
    all_to_all x0 -> x1, waiting for transfers between devices: none -> 349 us  [local(): lax.all_to_all(jnp.stack([w_qkv] * lax.axis_size('seq')), 'seq', 0, 0)]
    all_gather x1 -> x0, waiting for transfers between devices: 209 us -> none  [local(): lax.all_gather(w_qkv, 'seq', axis=0, tiled=True)]
    psum x1, blocking collectives: 40.5 us -> 117 us  [local(): numer, denom = lax.psum((gap, base_sum), ('seq', 'tp'))]
    all_to_all x0 -> x1, local copies, waits for them, and re-layouts: none -> 9.54 us  [local(): lax.all_to_all(jnp.stack([w_qkv] * lax.axis_size('seq')), 'seq', 0, 0)]
    all_to_all x0 -> x1, starting transfers between devices: none -> 8.53 us  [local(): lax.all_to_all(jnp.stack([w_qkv] * lax.axis_size('seq')), 'seq', 0, 0)]
    another operation x0 -> x1, local copies, waits for them, and re-layouts: none -> 7.56 us  [local(): jnp.stack([w_qkv] * lax.axis_size('seq'))]
  transfers between devices with their start and end apart: 3 -> 3, of which waited for: 3 -> 3; matrix products, arithmetic and copies ran while one was open for 2% -> 1% of each run, Pallas kernels for 0% -> 0%
where the time goes in v1:
time: 671 us; the launch traced here: 670 us
  waiting for transfers between devices  445 us (66%)
  blocking collectives  121 us (18%)
  local copies, waits for them, and re-layouts  51.9 us (8%)
  matrix products  18.6 us (3%)
  between operations  14.4 us (2%)
  other arithmetic  10.8 us (2%)
  starting transfers between devices  8.61 us (1%)
    all_to_all x1, waiting for transfers between devices, local(): lax.all_to_all(jnp.stack([w_qkv] * lax.axis_size('seq')), 'seq', 0, 0)  349 us
    psum x1, blocking collectives, local(): numer, denom = lax.psum((gap, base_sum), ('seq', 'tp'))  117 us
    all_gather x1, waiting for transfers between devices, local(): piece = lax.all_gather(paired, 'seq', axis=1, tiled=True)  79.9 us
    psum x1, waiting for transfers between devices, local(): lax.psum(partial_output.astype(jnp.bfloat16), 'tp').astype(jnp.float32)  16.1 us
  transfers between devices with their start and end apart: 3, of which 3 were waited for; matrix products, arithmetic and copies ran while one was open for 1% of the time, Pallas kernels for 0%

profile of v1, /device:TPU:0, one launch (start us, length us, event | category | flops | bytes accessed | tf_op | source)
XLA Modules:
  0.0 670.3 jit_solution(8741818420026604432)
XLA Ops:
  7.2 7.6 %stack.4 = bf16[16,192,3,1024]{3,1,2,0:T(8,128)(2,1)} broadcast(bf16[192,3,1024]{2,0,1:T(8,128)(2,1)} %param.15), dimensions={1,2,3} | broadcast | bytes 20054016 | tf_op jit(solution)/shard_map/stack | solution.py:47
  14.7 8.5 %all-to-all-start = ((bf16[16,192,3,1024]{3,1,2,0:T(8,128)(2,1)}), bf16[16,192,3,1024]{3,1,2,0:T(8,128)(2,1)}, u32[]{:S(2)}, u32[]{:S(2)}) async-start(bf16[16,192,3,1024]{3,1,2,0:T(8,128)(2,1)} %stack.4), calls=%async_computation | async-start | bytes 37748736 | tf_op jit(solution)/shard_map/all_to_all | solution.py:47
  23.3 0.0 all-gather.2.cloned.1.call-start
  23.3 1.9 all_gather.10
  25.2 0.1 pad_maximum_fusion.1
  25.4 2.5 all_gather.9
  27.9 0.2 convert_reduce_fusion
  28.1 0.4 fusion.12
  28.6 0.5 fusion.15
  29.1 348.7 %all-to-all-done = bf16[16,192,3,1024]{3,1,2,0:T(8,128)(2,1)} async-done(((bf16[16,192,3,1024]{3,1,2,0:T(8,128)(2,1)}), bf16[16,192,3,1024]{3,1,2,0:T(8,128)(2,1)}, u32[]{:S(2)}, u32[]{:S(2)}) %all-to-all-start) | async-done | bytes 18874400 | tf_op jit(solution)/shard_map/all_to_all | solution.py:47
  377.7 9.5 %copy.49 = bf16[16,192,3,1024]{3,1,0,2:T(8,128)(2,1)S(1)} copy(bf16[16,192,3,1024]{3,1,2,0:T(8,128)(2,1)} %all-to-all-done) | data formatting | bytes 37748736 | tf_op jit(solution)/shard_map/all_to_all | solution.py:47
  387.3 3.4 fusion.44
  390.7 0.8 slice.62
  391.5 0.9 slice_multiply_fusion
  392.4 1.2 reshape.136
  393.6 0.9 reduce_sum.66
  394.4 1.0 copy.51
  395.4 0.1 copy.52
  395.5 1.0 mul.103
  396.6 1.3 mul.104
  397.8 0.4 fusion.50
  398.2 1.1 pad_maximum_fusion
  399.3 1.3 copy.54
  400.6 0.0 all-gather.2.cloned.1.call-update
  400.6 0.0 all-reduce.3.cloned.1.call-start
  400.7 1.1 slice.53
  401.8 1.3 fusion.48
  403.1 117.1 %all-reduce = (f32[4]{0:T(128)S(1)}, f32[4]{0:T(128)S(1)}) all-reduce(f32[4]{0:T(128)S(1)} %get-tuple-element.4, f32[4]{0:T(128)S(1)} %get-tuple-element.3), channel_id=1, replica_groups=mesh['seq'=16,'tp'=2] {'seq','tp'}, use_global_device_ids=true, to_apply=%region_8.9 | all-reduce | flops 8 | bytes 64 | tf_op jit(solution)/shard_map/psum | solution.py:40
  520.2 0.1 compare_or_fusion
  520.2 0.1 slice.48
  520.3 0.1 copy.70
  520.4 0.2 fusion.51
  520.6 0.2 fusion.53
  520.9 79.9 %all-gather.2.cloned.1.call-done = bf16[4,576,2,1024]{3,0,2,1:T(4,128)(2,1)} async-done(((bf16[4,36,2,1024]{3,0,2,1:T(4,128)(2,1)}), bf16[4,576,2,1024]{3,0,2,1:T(4,128)(2,1)}) %all-gather.2.cloned.1.call-update) | async-done | bytes 9437200 | tf_op jit(solution)/shard_map/all_gather | solution.py:59
  600.7 10.7 %fusion.69 = (bf16[4,576,1,1024]{3,0,2,1:T(4,128)(2,1)}, bf16[4,576,1,1024]{3,0,2,1:T(4,128)(2,1)}) fusion(bf16[4,576,2,1024]{3,0,2,1:T(4,128)(2,1)} %all-gather.2.cloned.1.call-done), kind=kLoop, calls=%fused_computation.81 | loop fusion | bytes 18874368 | tf_op jit(solution)/shard_map/slice | solution.py:66
  611.4 8.0 %reshape.138 = bf16[4,576,8,128]{3,2,0,1:T(8,128)(2,1)} reshape(bf16[4,576,1,1024]{3,0,2,1:T(4,128)(2,1)} %get-tuple-element.10) | data formatting | bytes 9437184 | tf_op jit(solution)/shard_map/reshape;squeeze | solution.py:67
  619.4 8.2 %reshape.137 = bf16[4,576,8,128]{3,2,0,1:T(8,128)(2,1)} reshape(bf16[4,576,1,1024]{3,0,2,1:T(4,128)(2,1)} %get-tuple-element.9) | data formatting | bytes 9437184 | tf_op jit(solution)/shard_map/reshape;squeeze | solution.py:66
  627.6 7.7 %fusion.11 = (f32[4,8,32]{2,1,0:T(8,128)S(1)}, f32[4,8,32,576]{3,2,1,0:T(8,128)S(1)}) fusion(pred[4,576]{1,0:T(4,128)(4,1)S(1)} %compare_or_fusion, bf16[4,576,8,128]{3,2,0,1:T(8,128)(2,1)} %reshape.137, bf16[4,32,8,128]{3,2,1,0:T(8,128)(2,1)S(1)} %fusion.53), kind=kOutput, calls=%fused_computation.13 | convolution fusion | flops 152763392 | bytes 7346432 | tf_op jit(solution)/shard_map/bqhc,bkhc->bhqk/dot_general | solution.py:69
  635.2 0.0 slice-start
  635.3 0.8 fusion.16
  636.1 0.0 slice-start.1
  636.1 5.6 fusion.39
  641.8 1.9 fusion.6
  643.7 0.0 all-reduce.3.cloned.1.call-update
  643.7 0.5 maximum_divide_fusion
  644.3 0.7 bitcast_convert_fusion
  645.0 16.1 %all-reduce.3.cloned.1.call-done = bf16[4,32,3072]{2,1,0:T(8,128)(2,1)} async-done(((bf16[4,32,3072]{2,1,0:T(8,128)(2,1)}), bf16[4,32,3072]{2,1,0:T(8,128)(2,1)}) %all-reduce.3.cloned.1.call-update) | async-done | bytes 786448 | tf_op jit(solution)/shard_map/psum | solution.py:90
  661.0 2.4 convert_add_fusion
  (37 shorter events, 0.2 us)
Async XLA Ops:
  14.7 8.6 %copy-start.4 = (bf16[3,4,1536]{2,1,0:T(4,128)(2,1)S(1)}, bf16[3,4,1536]{2,1,0:T(4,128)(2,1)}, u32[]{:S(2)}) copy-start(bf16[3,4,1536]{2,1,0:T(4,128)(2,1)} %param.14) | copy-start | bytes 110596
  14.7 10.5 %copy-start = (bf16[4,32,1536]{2,1,0:T(8,128)(2,1)S(1)}, bf16[4,32,1536]{2,1,0:T(8,128)(2,1)}, u32[]{:S(2)}) copy-start(bf16[4,32,1536]{2,1,0:T(8,128)(2,1)} %param.10) | copy-start | bytes 1179652
  14.7 10.5 %copy-start.5 = (bf16[4,4,1536]{2,1,0:T(4,128)(2,1)S(1)}, bf16[4,4,1536]{2,1,0:T(4,128)(2,1)}, u32[]{:S(2)}) copy-start(bf16[4,4,1536]{2,1,0:T(4,128)(2,1)} %param.11) | copy-start | bytes 147460
  14.7 363.0 %all-to-all-start = ((bf16[16,192,3,1024]{3,1,2,0:T(8,128)(2,1)}), bf16[16,192,3,1024]{3,1,2,0:T(8,128)(2,1)}, u32[]{:S(2)}, u32[]{:S(2)}) async-start(bf16[16,192,3,1024]{3,1,2,0:T(8,128)(2,1)} %stack.4), calls=%async_computation | async-start | bytes 37748736 | tf_op jit(solution)/shard_map/all_to_all | solution.py:47
  23.3 5.3 copy-start.6
  23.3 577.4 %all-gather.2.cloned.1.call-start = ((), (), s32[]{:S(2)}) async-start(), calls=%async_computation.1 | async-start | bytes 10027008 | tf_op jit(solution)/shard_map/all_gather | solution.py:59
  398.2 3.6 copy-start.3
  398.2 121.9 %copy-start.7 = (s32[4]{0:T(128)S(1)}, s32[4]{0:T(128)}, u32[]{:S(2)}) copy-start(s32[4]{0:T(128)} %param.18) | copy-start | bytes 52
  400.6 260.4 %all-reduce.3.cloned.1.call-start = ((), (), s32[]{:S(2)}) async-start(), calls=%async_computation.2 | async-start | bytes 1572864 | tf_op jit(solution)/shard_map/psum | solution.py:90
  619.4 16.7 %slice-start.2 = ((s8[4718592]{0:T(1024)(128)(4,1)}), s8[524288]{0:T(1024)(128)(4,1)S(1)}, s32[]{:S(2)}) async-start(s8[4718592]{0:T(1024)(128)(4,1)} %bitcast.66), calls=%async_computation.5 | async-start | bytes 1048576
  627.6 8.5 %slice-start.3 = ((s8[4718592]{0:T(1024)(128)(4,1)}), s8[4194304]{0:T(1024)(128)(4,1)S(1)}, s32[]{:S(2)}) async-start(s8[4718592]{0:T(1024)(128)(4,1)} %bitcast.66), calls=%async_computation.6 | async-start | bytes 8388608
  635.2 6.5 slice-start
  636.1 5.7 slice-start.1
  641.8 1.9 copy-start.8
  641.8 19.2 %copy-start.1 = (bf16[4,32,1536]{2,1,0:T(8,128)(2,1)S(1)}, bf16[4,32,1536]{2,1,0:T(8,128)(2,1)}, u32[]{:S(2)}) copy-start(bf16[4,32,1536]{2,1,0:T(8,128)(2,1)} %param.10) | copy-start | bytes 1179652
  641.8 19.2 %copy-start.2 = (f32[4,32,1536]{2,1,0:T(8,128)S(1)}, f32[4,32,1536]{2,1,0:T(8,128)}, u32[]{:S(2)}) copy-start(f32[4,32,1536]{2,1,0:T(8,128)} %param.13) | copy-start | bytes 2359300
Sparse Core Ops, SparseCore 0:
  400.7 199.9 all-gather.1
  643.8 17.1 all-reduce.2
